TPU v7x, 32 devices: a whole 2x2x4 slice. The times are simulated.
32 devices in a mesh: row: 4 (over z), col: 8 (over y, x, core).
Axes of the slice: x: 2, y: 2, z: 4, core: 2. Of those that a mesh axis runs over, the one named last changes fastest.
Arguments:
- grad_terms: bfloat16 [8, 2, 4096, 10240], P('col', None, 'row'), may hold values from -25 to 25, as said below
- row_moment: float32 [2, 4096], P(None, 'row'), may hold values from 0.01 to 3
- col_moment: float32 [2, 10240], P(None, 'col'), may hold values from 0.01 to 1
Outputs:
- update: float32 [2, 4096, 10240], P(None, 'row', 'col')
- new_rows: float32 [2, 4096], P(None, 'row')
- new_cols: float32 [2, 10240], P(None, 'col')
Inputs may be any that keep to these rules, and one draw needn't show every extreme that they name: `grad_terms`: partial gradient terms of the 8 batch shards.
All inputs are finite; a program needn't handle non-finite values.
Results may differ from a plain program's by a relative error of at most 0.0003.
Values sent between devices are 32-bit elements; how exact they have to be, the bound alone decides.
No kernel may reach another device: no remote copies, remote signals or barrier semaphores. Data moves between devices by JAX's collectives and lax.ppermute only.
A program may use at most 256 MiB of HBM per device.

v0:
```python
import jax
import jax.numpy as jnp
from jax import lax
from jax.sharding import PartitionSpec as P

D = 4096
FF = 10240
second_decay = 1.0 - 100.0 ** (-0.8)
tiny_square = 1e-30


def on_device(grad_terms, row_moment, col_moment):
    partial_terms = grad_terms[0]
    gradient = lax.psum_scatter(
        partial_terms.astype(jnp.float32), "col", scatter_dimension=2, tiled=True
    )
    squares = gradient * gradient + tiny_square
    row_part = jnp.sum(squares, axis=2)
    col_part = jnp.sum(squares, axis=1)
    row_full = lax.psum(row_part, "col")
    col_full = lax.psum(col_part, "row")
    new_rows = second_decay * row_moment + (1.0 - second_decay) * row_full / FF
    new_cols = second_decay * col_moment + (1.0 - second_decay) * col_full / D
    row_level = lax.psum(jnp.sum(new_rows, axis=1), "row") / D
    estimate = new_rows[:, :, None] * new_cols[:, None, :] / row_level[:, None, None]
    raw_update = gradient / jnp.sqrt(estimate)
    clip_total = lax.psum(jnp.sum(raw_update * raw_update, axis=(1, 2)), ("row", "col"))
    clip_scale = jnp.maximum(1.0, jnp.sqrt(clip_total / (D * FF)))
    update = raw_update / clip_scale[:, None, None]
    return (update, new_rows, new_cols)


def solution(mesh):
    placed = (P("col", None, "row", None), P(None, "row"), P(None, "col"))
    return jax.shard_map(
        on_device,
        mesh=mesh,
        in_specs=placed,
        out_specs=(P(None, "row", "col"), P(None, "row"), P(None, "col")),
        check_vma=False,
    )
```

profile of v0, /device:TPU:10, one launch (start us, length us, event | category | flops | bytes accessed | tf_op | source)
XLA Modules:
  0.0 610.9 jit_solution(3607653950137789142)
XLA Ops:
  7.2 0.0 reduce-scatter.2.cloned.1.call-start
  7.2 40.9 %bitcast_convert_fusion = f32[2,1024,10240]{2,1,0:T(8,128)} fusion(bf16[1,2,1024,10240]{3,2,1,0:T(8,128)(2,1)} %param.3), kind=kLoop, calls=%fused_computation | loop fusion | flops 20971520 | bytes 125829120 | tf_op jit(solution)/shard_map/convert_element_type | solution.py:15
  48.1 0.0 reduce-scatter.2.cloned.1.call-update
  48.1 0.0 copy-start.3
  48.1 0.0 copy-start.2
  48.1 464.0 %reduce-scatter.2.cloned.1.call-done = f32[2,1024,1280]{2,1,0:T(8,128)} async-done(((f32[2,1024,10240]{2,1,0:T(8,128)}), f32[2,1024,1280]{2,1,0:T(8,128)}) %reduce-scatter.2.cloned.1.call-update) | async-done | bytes 10485776 | tf_op jit(solution)/shard_map/reduce_scatter | solution.py:14
  512.1 5.8 fusion
  517.9 10.3 %psum.28 = f32[2,1024]{1,0:T(2,128)S(1)} all-reduce(f32[2,1024]{1,0:T(2,128)S(1)} %get-tuple-element.4), channel_id=1, replica_groups=mesh['row'=4,'col'=8] {'col'}, use_global_device_ids=true, to_apply=%region_2.0 | all-reduce | flops 2048 | bytes 16384 | tf_op jit(solution)/shard_map/psum | solution.py:20
  528.1 0.0 copy-done.3
  528.1 0.1 fusion.2
  528.3 0.0 copy-start.1
  528.3 15.1 %all-reduce = (f32[2]{0:T(128)S(1)}, f32[2,1280]{1,0:T(2,128)S(1)}) all-reduce(f32[2]{0:T(128)S(1)} %get-tuple-element.7, f32[2,1280]{1,0:T(2,128)S(1)} %get-tuple-element.3), channel_id=1, replica_groups=mesh['row'=4,'col'=8] {'row'}, use_global_device_ids=true, to_apply=%region_6.0 | all-reduce | flops 2562 | bytes 20496 | tf_op jit(solution)/shard_map/psum | solution.py:24
  543.4 0.0 copy-done.2
  543.4 0.0 copy-start
  543.4 5.9 multiply_reduce_fusion
  549.4 45.0 %psum.31 = f32[2]{0:T(128)S(1)} all-reduce(f32[2]{0:T(128)S(1)} %multiply_reduce_fusion), channel_id=1, replica_groups=mesh['row'=4,'col'=8] {'row','col'}, use_global_device_ids=true, to_apply=%region_8.0 | all-reduce | flops 2 | bytes 16 | tf_op jit(solution)/shard_map/psum | solution.py:27
  594.4 9.6 %broadcast_divide_fusion = f32[2,1024,1280]{2,1,0:T(8,128)} fusion(f32[2]{0:T(128)S(1)} %sqrt_maximum_fusion, f32[2,1024,1280]{2,1,0:T(8,128)} %reduce-scatter.2.cloned.1.call-done, f32[2]{0:T(128)S(1)} %broadcast_multiply_fusion, f32[2,1280]{1,0:T(2,128)S(1)} %multiply_add_fusion.1, f32[2,1024]{1,0:T(2,128)S(1)} %get-tuple-element.8), kind=kLoop, calls=%fused_computation.6 | loop fusion | flops 10485760 | bytes 20989968 | tf_op jit(solution)/shard_map/div | solution.py:29
  604.0 0.0 copy-done.1
  604.0 0.0 copy-done
  (3 shorter events, 0.0 us)
Async XLA Ops:
  7.2 504.9 %reduce-scatter.2.cloned.1.call-start = ((), (), s32[]{:S(2)}) async-start(), calls=%async_computation.1 | async-start | bytes 94371840 | tf_op jit(solution)/shard_map/reduce_scatter | solution.py:14
  48.1 480.0 %copy-start.3 = (f32[2,1024]{1,0:T(2,128)S(1)}, f32[2,1024]{1,0:T(2,128)}, u32[]{:S(2)}) copy-start(f32[2,1024]{1,0:T(2,128)} %param.4) | copy-start | bytes 24580
  48.1 495.3 %copy-start.2 = (f32[2,1280]{1,0:T(2,128)S(1)}, f32[2,1280]{1,0:T(2,128)}, u32[]{:S(2)}) copy-start(f32[2,1280]{1,0:T(2,128)} %param.5) | copy-start | bytes 30724
  528.3 75.7 %copy-start.1 = (f32[2,1024]{1,0:T(2,128)}, f32[2,1024]{1,0:T(2,128)S(1)}, u32[]{:S(2)}) copy-start(f32[2,1024]{1,0:T(2,128)S(1)} %get-tuple-element.8) | copy-start | bytes 24580
  543.4 60.6 %copy-start = (f32[2,1280]{1,0:T(2,128)}, f32[2,1280]{1,0:T(2,128)S(1)}, u32[]{:S(2)}) copy-start(f32[2,1280]{1,0:T(2,128)S(1)} %multiply_add_fusion.1) | copy-start | bytes 30724
Sparse Core Ops, SparseCore 0:
  48.2 463.8 reduce-scatter.1
where the time goes:
time: 611 us
  waiting for transfers between devices  464 us (76%)
  blocking collectives  70.4 us (12%)
  other arithmetic  62.3 us (10%)
  between operations  14.1 us (2%)
    reduce_scatter x1, waiting for transfers between devices, on_device(): lax.psum_scatter(partial_terms.astype(jnp.float32), 'col', scatter_dimens...  464 us
    psum x1, blocking collectives, on_device(): lax.psum(jnp.sum(raw_update * raw_update, axis=(1, 2)), ('row', 'col'))  45 us
    convert_element_type x1, other arithmetic, on_device(): partial_terms.astype(jnp.float32)  40.9 us
    psum x1, blocking collectives, on_device(): row_level = lax.psum(jnp.sum(new_rows, axis=1), 'row') / D  15.1 us
  transfers between devices with their start and end apart: 1, of which 1 were waited for; matrix products, arithmetic and copies ran while one was open for 0% of the time, Pallas kernels for 0%

commit v1 on v0

--- a/solution.py
+++ b/solution.py
@@ -24,7 +24,7 @@
     row_level = lax.psum(jnp.sum(new_rows, axis=1), "row") / D
     estimate = new_rows[:, :, None] * new_cols[:, None, :] / row_level[:, None, None]
     raw_update = gradient / jnp.sqrt(estimate)
-    clip_total = lax.psum(jnp.sum(raw_update * raw_update, axis=(1, 2)), ("row", "col"))
+    clip_total = lax.psum(lax.psum(jnp.sum(raw_update * raw_update, axis=(1, 2)), "row"), "col")
     clip_scale = jnp.maximum(1.0, jnp.sqrt(clip_total / (D * FF)))
     update = raw_update / clip_scale[:, None, None]
     return (update, new_rows, new_cols)

time: 611 us -> 594 us (0.972)
  blocking collectives: 70.4 us -> 49.9 us
    psum x1 -> x2, blocking collectives: 45 us -> 24.5 us  [the longest x1 12.4 us: on_device(): lax.psum(jnp.sum(raw_update * raw_update, axis=(1, 2)), 'row')]
where the time goes in v1:
time: 594 us; the launch traced here: 590 us
  waiting for transfers between devices  464 us (78%)
  other arithmetic  62.3 us (10%)
  blocking collectives  49.9 us (8%)
  between operations  14.1 us (2%)
    reduce_scatter x1, waiting for transfers between devices, on_device(): lax.psum_scatter(partial_terms.astype(jnp.float32), 'col', scatter_dimens...  464 us
    convert_element_type x1, other arithmetic, on_device(): partial_terms.astype(jnp.float32)  40.9 us
    psum x1, blocking collectives, on_device(): row_level = lax.psum(jnp.sum(new_rows, axis=1), 'row') / D  15.1 us
    psum x1, blocking collectives, on_device(): lax.psum(jnp.sum(raw_update * raw_update, axis=(1, 2)), 'row')  12.4 us
    psum x1, blocking collectives, on_device(): lax.psum(lax.psum(jnp.sum(raw_update * raw_update, axis=(1, 2)), 'row'),...  12.1 us
  transfers between devices with their start and end apart: 1, of which 1 were waited for; matrix products, arithmetic and copies ran while one was open for 0% of the time, Pallas kernels for 0%

profile of v1, /device:TPU:10, one launch (start us, length us, event | category | flops | bytes accessed | tf_op | source)
XLA Modules:
  0.0 590.3 jit_solution(5969502915394997094)
XLA Ops:
  7.2 0.0 reduce-scatter.2.cloned.1.call-start
  7.2 40.9 %bitcast_convert_fusion = f32[2,1024,10240]{2,1,0:T(8,128)} fusion(bf16[1,2,1024,10240]{3,2,1,0:T(8,128)(2,1)} %param.3), kind=kLoop, calls=%fused_computation | loop fusion | flops 20971520 | bytes 125829120 | tf_op jit(solution)/shard_map/convert_element_type | solution.py:15
  48.1 0.0 reduce-scatter.2.cloned.1.call-update
  48.1 0.0 copy-start.3
  48.1 0.0 copy-start.2
  48.1 464.0 %reduce-scatter.2.cloned.1.call-done = f32[2,1024,1280]{2,1,0:T(8,128)} async-done(((f32[2,1024,10240]{2,1,0:T(8,128)}), f32[2,1024,1280]{2,1,0:T(8,128)}) %reduce-scatter.2.cloned.1.call-update) | async-done | bytes 10485776 | tf_op jit(solution)/shard_map/reduce_scatter | solution.py:14
  512.1 5.8 fusion
  517.9 10.3 %psum.35 = f32[2,1024]{1,0:T(2,128)S(1)} all-reduce(f32[2,1024]{1,0:T(2,128)S(1)} %get-tuple-element.4), channel_id=1, replica_groups=mesh['row'=4,'col'=8] {'col'}, use_global_device_ids=true, to_apply=%region_2.0 | all-reduce | flops 2048 | bytes 16384 | tf_op jit(solution)/shard_map/psum | solution.py:20
  528.1 0.0 copy-done.3
  528.1 0.1 fusion.2
  528.3 0.0 copy-start.1
  528.3 15.1 %all-reduce = (f32[2]{0:T(128)S(1)}, f32[2,1280]{1,0:T(2,128)S(1)}) all-reduce(f32[2]{0:T(128)S(1)} %get-tuple-element.7, f32[2,1280]{1,0:T(2,128)S(1)} %get-tuple-element.3), channel_id=1, replica_groups=mesh['row'=4,'col'=8] {'row'}, use_global_device_ids=true, to_apply=%region_6.0 | all-reduce | flops 2562 | bytes 20496 | tf_op jit(solution)/shard_map/psum | solution.py:24
  543.4 0.0 copy-done.2
  543.4 0.0 copy-start
  543.4 5.9 %multiply_reduce_fusion = f32[2]{0:T(128)S(1)} fusion(f32[2,1024,1280]{2,1,0:T(8,128)} %reduce-scatter.2.cloned.1.call-done, f32[2]{0:T(128)S(1)} %broadcast_multiply_fusion, f32[2,1280]{1,0:T(2,128)S(1)} %multiply_add_fusion.1, f32[2,1024]{1,0:T(2,128)S(1)} %get-tuple-element.8), kind=kLoop, calls=%fused_computation.1 | loop fusion | flops 13107198 | bytes 10504208 | tf_op jit(solution)/shard_map/reduce_sum | solution.py:27
  549.4 12.4 %psum.38 = f32[2]{0:T(128)S(1)} all-reduce(f32[2]{0:T(128)S(1)} %multiply_reduce_fusion), channel_id=1, replica_groups=mesh['row'=4,'col'=8] {'row'}, use_global_device_ids=true, to_apply=%region_8.0 | all-reduce | flops 2 | bytes 16 | tf_op jit(solution)/shard_map/psum | solution.py:27
  561.7 12.1 %psum.39 = f32[2]{0:T(128)S(1)} all-reduce(f32[2]{0:T(128)S(1)} %psum.38), channel_id=1, replica_groups=mesh['row'=4,'col'=8] {'col'}, use_global_device_ids=true, to_apply=%region_9.0 | all-reduce | flops 2 | bytes 16 | tf_op jit(solution)/shard_map/psum | solution.py:27
  573.9 9.6 %broadcast_divide_fusion = f32[2,1024,1280]{2,1,0:T(8,128)} fusion(f32[2]{0:T(128)S(1)} %sqrt_maximum_fusion, f32[2,1024,1280]{2,1,0:T(8,128)} %reduce-scatter.2.cloned.1.call-done, f32[2]{0:T(128)S(1)} %broadcast_multiply_fusion, f32[2,1280]{1,0:T(2,128)S(1)} %multiply_add_fusion.1, f32[2,1024]{1,0:T(2,128)S(1)} %get-tuple-element.8), kind=kLoop, calls=%fused_computation.6 | loop fusion | flops 10485760 | bytes 20989968 | tf_op jit(solution)/shard_map/div | solution.py:29
  583.5 0.0 copy-done.1
  583.5 0.0 copy-done
  (3 shorter events, 0.0 us)
Async XLA Ops:
  7.2 504.9 %reduce-scatter.2.cloned.1.call-start = ((), (), s32[]{:S(2)}) async-start(), calls=%async_computation.1 | async-start | bytes 94371840 | tf_op jit(solution)/shard_map/reduce_scatter | solution.py:14
  48.1 480.0 %copy-start.3 = (f32[2,1024]{1,0:T(2,128)S(1)}, f32[2,1024]{1,0:T(2,128)}, u32[]{:S(2)}) copy-start(f32[2,1024]{1,0:T(2,128)} %param.4) | copy-start | bytes 24580
  48.1 495.3 %copy-start.2 = (f32[2,1280]{1,0:T(2,128)S(1)}, f32[2,1280]{1,0:T(2,128)}, u32[]{:S(2)}) copy-start(f32[2,1280]{1,0:T(2,128)} %param.5) | copy-start | bytes 30724
  528.3 55.2 %copy-start.1 = (f32[2,1024]{1,0:T(2,128)}, f32[2,1024]{1,0:T(2,128)S(1)}, u32[]{:S(2)}) copy-start(f32[2,1024]{1,0:T(2,128)S(1)} %get-tuple-element.8) | copy-start | bytes 24580
  543.4 40.0 %copy-start = (f32[2,1280]{1,0:T(2,128)}, f32[2,1280]{1,0:T(2,128)S(1)}, u32[]{:S(2)}) copy-start(f32[2,1280]{1,0:T(2,128)S(1)} %multiply_add_fusion.1) | copy-start | bytes 30724
Sparse Core Ops, SparseCore 0:
  48.2 463.8 reduce-scatter.1
